TPU v7x, 32 devices: a whole 2x2x4 slice. The times are simulated.
32 devices in a mesh: gx: 4 (over y, x), gy: 2 (over core), gz: 4 (over z).
Axes of the slice: x: 2, y: 2, z: 4, core: 2. Of those that a mesh axis runs over, the one named last changes fastest.
Arguments:
- star_residual: bfloat16 [128, 64, 1152], P(('gx', 'gy', 'gz')), may hold values from -6 to 6
- patch_inverse: bfloat16 [128, 1152, 1152], P(('gx', 'gy', 'gz')), may hold values from -0.1875 to 0.1875
- block_owner: int32 [128, 9], P(('gx', 'gy', 'gz')), may hold values from 0 to 31, as said below
- block_slot: int32 [128, 9], P(('gx', 'gy', 'gz')), may hold values from 0 to 1, as said below
- recv_target: int32 [32, 27, 2], P(('gx', 'gy', 'gz')), may hold values from -1 to 7, as said below
Outputs:
- owned_sum: float32 [256, 64, 128], P(('gx', 'gy', 'gz'))
- combined: float32 [128, 9, 64, 128], P(('gx', 'gy', 'gz'))
Inputs may be any that keep to these rules, and one draw needn't show every extreme that they name: `block_owner`: each block's owner is the block's own partition or one whose coordinate differs by at most one step along each of the three mesh axes, counted with wrap-around. `block_slot`: blocks of one partition that have the same owner have distinct slots; in every partition some owner receives exactly 2 of its blocks. `recv_target`: every slot that a block uses maps to an owned block of its owner; slots that no block uses hold -1.
All inputs are finite; a program needn't handle non-finite values.
Results may differ from a plain program's by a relative error of at most 0.0003.
Values sent between devices are 32-bit elements; how exact they have to be, the bound alone decides.
A program may use at most 64 MiB of HBM per device.

v0:
```python
import functools

import jax
import jax.numpy as jnp
from jax import lax
from jax.experimental import pallas as pl
from jax.experimental.pallas import tpu as pltpu
from jax.sharding import PartitionSpec as P

OWNB = 8
CHUNKS = 2
MESH = pl.DeviceIdType.MESH


def offsets(extent):
    return [0, 1, -1][: min(extent, 3)]


def offset_index(far, near, extent):
    distance = lax.rem(far - near + extent, extent)
    return jnp.where(distance <= 1, distance, 2)


def slot_of(owner, block_slot, extents, capacity):
    nx, ny, nz = extents
    gx, gy, gz = lax.axis_index("gx"), lax.axis_index("gy"), lax.axis_index("gz")
    at_x = offset_index(lax.div(owner, ny * nz), gx, nx)
    role = jnp.where((at_x > 0) & (lax.rem(gx, 2) == 1), 3 - at_x, at_x)
    at_y = offset_index(lax.rem(lax.div(owner, nz), ny), gy, ny)
    at_z = offset_index(lax.rem(owner, nz), gz, nz)
    return ((at_y * len(offsets(nz)) + at_z) * 3 + role) * capacity + block_slot


def code_of(offset):
    return offset + 1


def gather_kernel(cfg, owner_ref, slot_ref, held_ref, back_ref, owned_ref, comb_ref,
                  own, comb, in_sem, out_sem):
    extents, capacity = cfg
    patch_count, block_count = owner_ref.shape
    own_in = pltpu.make_async_copy(held_ref, own, in_sem.at[patch_count])
    own_out = pltpu.make_async_copy(own, owned_ref, out_sem.at[patch_count])
    own_in.start()
    for p in range(patch_count):
        def fetch(b, carry):
            k = slot_of(owner_ref[p, b], slot_ref[p, b], extents, capacity)
            pltpu.make_async_copy(back_ref.at[k], comb.at[p, b], in_sem.at[p]).start()
            return carry
        lax.fori_loop(0, block_count, fetch, 0, unroll=True)
    own_in.wait()
    own_out.start()
    outs = [own_out]
    for p in range(patch_count):
        pltpu.make_async_copy(back_ref.at[pl.ds(0, block_count)], comb.at[p], in_sem.at[p]).wait()
        out = pltpu.make_async_copy(comb.at[p], comb_ref.at[p], out_sem.at[p])
        out.start()
        outs.append(out)
    for out in outs:
        out.wait()


def kernel(cfg, owner_ref, slot_ref, table_ref, star_ref, inv_hbm, owned_ref, back,
           star, inv, key_ref, src_ref, sent, came, tgt_out, tgt, pd, px, ry, rx, own, g1, g2, ans,
           own_sem, self_sem, load_sem, tgt_send, tgt_recv, a_send, a_recv, y_send, y_recv, x_send, x_recv,
           g_send, g_recv, h_send, h_recv, b_send, b_recv):
    nx, ny, nz, chunks, block_count, capacity = cfg
    gx, gy, gz = lax.axis_index("gx"), lax.axis_index("gy"), lax.axis_index("gz")
    patch_count = inv_hbm.shape[0] // block_count
    total = inv_hbm.shape[0]
    rows = came.shape[2]
    lanes = came.shape[3]
    pairs = [(dy, dz) for dy in offsets(ny) for dz in offsets(nz)]
    count = len(pairs)
    far = sorted(range(1, count), key=lambda q: pairs[q][1] == 0)
    near_x = (gx + 1 - 2 * (gx % 2), gy, gz)
    near_y = ((gx + 2) % 4, gy, gz)
    corner = (3 - gx, gy, gz)

    def ahead(q):
        return (gx, (gy + pairs[q][0] + ny) % ny, (gz + pairs[q][1] + nz) % nz)

    def behind(q):
        return (gx, (gy - pairs[q][0] + ny) % ny, (gz - pairs[q][1] + nz) % nz)

    loads = [pltpu.make_async_copy(star_ref, star, load_sem.at[patch_count])]
    for p in range(patch_count):
        part = pl.ds(p * block_count, block_count)
        loads.append(pltpu.make_async_copy(inv_hbm.at[part], inv.at[part], load_sem.at[p]))
    for load in loads:
        load.start()

    barrier = pltpu.get_barrier_semaphore()
    greeted = [ahead(q) for q in range(1, count)] + [near_x, near_y, corner]
    for device in greeted:
        pl.semaphore_signal(barrier, inc=1, device_id=device, device_id_type=MESH)

    parity = gx % 2
    for role in range(3):
        code_x = (1, 2 * parity, 2 - 2 * parity)[role]
        held = tgt if role == 0 else tgt_out
        for q in range(count):
            code = 9 * code_x + 3 * code_of(pairs[q][0]) + code_of(pairs[q][1])
            for s in range(capacity):
                i = q * capacity + s
                held[role, i:i + 1, :] = jnp.full((1, lanes), table_ref[0, s, code], jnp.int32)

    def number(n, carry):
        p, b = lax.div(n, block_count), lax.rem(n, block_count)
        key_ref[n] = slot_of(owner_ref[p, b], slot_ref[p, b], (nx, ny, nz), capacity)
        return carry

    lax.fori_loop(0, total, number, 0)

    def invert(k, carry):
        found = jnp.int32(0)
        for n in range(total):
            found = jnp.where(key_ref[n] == k, n, found)
        src_ref[k] = found
        return carry

    lax.fori_loop(0, count * 3 * capacity, invert, 0)

    pl.semaphore_wait(barrier, len(greeted))

    sends = []

    def remote(source, target, send_sem, recv_sem, device):
        copy = pltpu.make_async_remote_copy(
            src_ref=source, dst_ref=target, send_sem=send_sem, recv_sem=recv_sem,
            device_id=device, device_id_type=MESH)
        return copy

    def launch(copy):
        copy.start()
        sends.append(copy)
        return copy

    tgt_copies = {}
    for role, device in ((1, near_x), (2, corner)):
        tgt_copies[role] = launch(remote(
            tgt_out.at[role], tgt.at[role], tgt_send.at[role - 1], tgt_recv.at[role - 1], device))

    def slot(q, role):
        return (q * 3 + role) * capacity

    def part(ref, c, q, role):
        return ref.at[c, pl.ds(slot(q, role), capacity)]

    for load in loads:
        load.wait()

    a_copies = {}
    for role in (2, 1, 0):
        for q in far + [0]:
            held = came if q == 0 else sent
            for s in range(capacity):
                k = slot(q, role) + s
                n = src_ref[k]
                block = lax.dot_general(
                    star[n // block_count], inv[n], (((1,), (1,)), ((), ())),
                    preferred_element_type=jnp.float32)
                for c in range(chunks):
                    held[c, k] = block[c * rows:(c + 1) * rows]
            if q:
                a_copies[q, role, 0] = launch(remote(
                    part(sent, 0, q, role), part(came, 0, q, role),
                    a_send.at[q, role, 0], a_recv.at[q, role, 0], ahead(q)))
        for c in range(1, chunks):
            for q in far:
                a_copies[q, role, c] = launch(remote(
                    part(sent, c, q, role), part(came, c, q, role),
                    a_send.at[q, role, c], a_recv.at[q, role, c], ahead(q)))

    tgt_copies[1].wait_recv()
    tgt_copies[2].wait_recv()

    def targets(role, i):
        return jnp.broadcast_to(tgt[role, i:i + 1, :], (8, lanes))

    def reduce(role, c, store):
        for q in far:
            a_copies[q, role, c].wait_recv()

        def body(r, carry):
            at = pl.ds(pl.multiple_of(r * 8, 8), 8)
            sums = [jnp.zeros((8, lanes), jnp.float32) for _ in range(OWNB)]
            for q in range(count):
                for s in range(capacity):
                    value = came[c, slot(q, role) + s, at, :]
                    where = targets(role, q * capacity + s)
                    for t in range(OWNB):
                        sums[t] = sums[t] + jnp.where(where == t, value, 0.0)
            for t in range(OWNB):
                store(t, at, r, sums[t])
            return carry

        lax.fori_loop(0, rows // 8, body, 0)

    b_copies = {}
    locals_ = []

    def landing(c, q, role):
        return back.at[pl.ds(slot(q, role), capacity), pl.ds(c * rows, rows)]

    def put(source, target, sem):
        copy = pltpu.make_async_copy(source, target, sem)
        copy.start()
        locals_.append(copy)

    def answer(role, c, held):
        def body(r, carry):
            at = pl.ds(pl.multiple_of(r * 8, 8), 8)
            values = [held[c, t, at, :] for t in range(OWNB)]
            for q in range(count):
                for s in range(capacity):
                    where = targets(role, q * capacity + s)
                    out = values[0]
                    for t in range(1, OWNB):
                        out = jnp.where(where == t, values[t], out)
                    ans[c, slot(q, role) + s, at, :] = out
            return carry

        lax.fori_loop(0, rows // 8, body, 0)
        put(part(ans, c, 0, role), landing(c, 0, role), self_sem.at[role, c])
        for q in far:
            b_copies[q, role, c] = launch(remote(
                part(ans, c, q, role), landing(c, q, role),
                b_send.at[q, role, c], b_recv.at[q, role, c], behind(q)))

    y_copies, x_copies, g_copies, h_copies = {}, {}, {}, {}

    def stage_corner(c):
        def store(t, at, r, value):
            pd[c, t, at, :] = value
        reduce(2, c, store)
        y_copies[c] = launch(remote(pd.at[c], ry.at[c], y_send.at[c], y_recv.at[c], near_y))

    def stage_near(c):
        y_copies[c].wait_recv()

        def store(t, at, r, value):
            px[c, t, at, :] = value + ry[c, t, at, :]
        reduce(1, c, store)
        x_copies[c] = launch(remote(px.at[c], rx.at[c], x_send.at[c], x_recv.at[c], near_x))

    def stage_own(c):
        x_copies[c].wait_recv()

        def store(t, at, r, value):
            own[c, t, at, :] = value + rx[c, t, at, :]
        reduce(0, c, store)
        g_copies[c] = launch(remote(own.at[c], g1.at[c], g_send.at[c], g_recv.at[c], near_x))
        put(own.at[c], owned_ref.at[:, pl.ds(c * rows, rows)], own_sem.at[c])
        answer(0, c, own)

    def stage_back_near(c):
        g_copies[c].wait_recv()
        h_copies[c] = launch(remote(g1.at[c], g2.at[c], h_send.at[c], h_recv.at[c], near_y))
        answer(1, c, g1)

    def stage_back_corner(c):
        h_copies[c].wait_recv()
        answer(2, c, g2)

    stages = [stage_corner, stage_near, stage_own, stage_back_near, stage_back_corner]
    steps = [(c + 2 * i, i, c) for i in range(len(stages)) for c in range(chunks)]
    for _, i, c in sorted(steps):
        stages[i](c)

    for copy in b_copies.values():
        copy.wait_recv()

    for copy in locals_:
        copy.wait()
    for copy in sends:
        copy.wait_send()


def on_device(star_residual, patch_inverse, block_owner, block_slot, recv_target):
    nx, ny, nz = lax.axis_size("gx"), lax.axis_size("gy"), lax.axis_size("gz")
    patch_count, rhs_count, patch_order = star_residual.shape
    block_count = block_owner.shape[1]
    width = patch_order // block_count
    capacity = recv_target.shape[2]
    total = patch_count * block_count
    ly, lz = len(offsets(ny)), len(offsets(nz))
    count = ly * lz
    slots = count * 3 * capacity
    chunks = CHUNKS
    rows = rhs_count // chunks
    smem = pl.BlockSpec(memory_space=pltpu.SMEM)
    anywhere = pl.BlockSpec(memory_space=pl.ANY)
    f32 = jnp.float32
    slotted = pltpu.VMEM((chunks, slots, rows, width), f32)
    targeted = pltpu.VMEM((chunks, OWNB, rows, width), f32)
    dma = pltpu.SemaphoreType.DMA
    held, back = pl.pallas_call(
        functools.partial(kernel, (nx, ny, nz, chunks, block_count, capacity)),
        out_shape=(
            jax.ShapeDtypeStruct((OWNB, rhs_count, width), f32),
            jax.ShapeDtypeStruct((slots, rhs_count, width), f32),
        ),
        in_specs=[smem, smem, smem, anywhere, anywhere],
        out_specs=(anywhere, anywhere),
        scratch_shapes=[
            pltpu.VMEM(star_residual.shape, star_residual.dtype),
            pltpu.VMEM((total, width, patch_order), patch_inverse.dtype),
            pltpu.SMEM((total,), jnp.int32),
            pltpu.SMEM((slots,), jnp.int32),
            slotted, slotted,
            pltpu.VMEM((3, count * capacity, width), jnp.int32),
            pltpu.VMEM((3, count * capacity, width), jnp.int32),
            targeted, targeted, targeted, targeted, targeted, targeted, targeted,
            slotted,
            dma((chunks,)), dma((3, chunks)),
            dma((patch_count + 1,)), dma((2,)), dma((2,)),
            dma((count, 3, chunks)), dma((count, 3, chunks)),
            dma((chunks,)), dma((chunks,)), dma((chunks,)), dma((chunks,)),
            dma((chunks,)), dma((chunks,)), dma((chunks,)), dma((chunks,)),
            dma((count, 3, chunks)), dma((count, 3, chunks)),
        ],
        compiler_params=pltpu.CompilerParams(
            collective_id=0, has_side_effects=True, vmem_limit_bytes=56 * 1024 * 1024),
    )(block_owner, block_slot, recv_target.transpose(0, 2, 1), star_residual,
      patch_inverse.reshape(total, width, patch_order))
    return pl.pallas_call(
        functools.partial(gather_kernel, ((nx, ny, nz), capacity)),
        out_shape=(
            jax.ShapeDtypeStruct((OWNB, rhs_count, width), f32),
            jax.ShapeDtypeStruct((patch_count, block_count, rhs_count, width), f32),
        ),
        in_specs=[smem, smem, anywhere, anywhere],
        out_specs=(anywhere, anywhere),
        scratch_shapes=[
            pltpu.VMEM((OWNB, rhs_count, width), f32),
            pltpu.VMEM((patch_count, block_count, rhs_count, width), f32),
            dma((patch_count + 1,)), dma((patch_count + 1,)),
        ],
    )(block_owner, block_slot, held, back)


def solution(mesh):
    placed = (
        P(("gx", "gy", "gz"), None, None),
        P(("gx", "gy", "gz"), None, None),
        P(("gx", "gy", "gz"), None),
        P(("gx", "gy", "gz"), None),
        P(("gx", "gy", "gz"), None, None),
    )
    return jax.shard_map(
        on_device,
        mesh=mesh,
        in_specs=placed,
        out_specs=(P(("gx", "gy", "gz"), None, None), P(("gx", "gy", "gz"), None, None, None)),
        check_vma=False,
    )
```

profile of v0, /device:TPU:0, one launch (start us, length us, event | category | flops | bytes accessed | tf_op | source)
XLA Modules:
  0.0 49.9 jit_solution(4576796447602681531)
XLA Ops:
  0.6 46.2 %shard_map.68 = (f32[8,64,128]{2,1,0:T(8,128)}, f32[36,64,128]{2,1,0:T(8,128)}) custom-call(s32[4,9]{1,0:T(4,128)} %owner_ref.3, s32[4,9]{1,0:T(4,128)} %slot_ref.3, s32[1,2,27]{2,1,0:T(2,128)} %bitcast.3, bf16[4,64,1152]{2,1,0:T(8,128)(2,1)} %star_ref.1, bf16[36,128,1152]{2,1,0:T(8,128)(2,1)} %bitcast.2), custom_call_target="tpu_custom_call" | custom-call | tf_op jit(solution)/shard_map/pallas_call | solution.py:298
  46.9 3.0 %shard_map.69 = (f32[8,64,128]{2,1,0:T(8,128)}, f32[4,9,64,128]{3,2,1,0:T(8,128)}) custom-call(s32[4,9]{1,0:T(4,128)} %owner_ref.3, s32[4,9]{1,0:T(4,128)} %slot_ref.3, f32[8,64,128]{2,1,0:T(8,128)} %get-tuple-element.4.held_ref, f32[36,64,128]{2,1,0:T(8,128)} %get-tuple-element.5.back_ref), custom_call_target="tpu_custom_call" | custom-call | tf_op jit(solution)/shard_map/pallas_call | solution.py:327
where the time goes:
time: 50.2 us; the launch traced here: 49.9 us
  Pallas kernels  49.3 us (98%)
  between operations  0.64 us (1%)
    pallas_call x1, Pallas kernels, on_device(): pl.pallas_call(functools.partial(kernel, (nx, ny, nz, chunks, block_count...  46.2 us
    pallas_call x1, Pallas kernels, on_device(): pl.pallas_call(functools.partial(gather_kernel, ((nx, ny, nz), capacity))...  3.01 us

commit v1 on v0

v1 whole, which is shorter than its diff:
```python
import functools

import jax
import jax.numpy as jnp
from jax import lax
from jax.experimental import pallas as pl
from jax.experimental.pallas import tpu as pltpu
from jax.sharding import PartitionSpec as P

OWNB = 8
CHUNKS = 4
VMEM_BYTES = 67043328
SPARE = 131072
MESH = pl.DeviceIdType.MESH


def offsets(extent):
    return [0, 1, -1][: min(extent, 3)]


def offset_index(far, near, extent):
    step = far - near
    distance = jnp.where(step < 0, step + extent, step)
    return jnp.where(distance <= 1, distance, 2)


def role_of(at, here):
    return jnp.where((at > 0) & (lax.rem(here, 2) == 1), 3 - at, at)


def partner(here, role, extent):
    step = 1 - 2 * (here % 2)
    return (here + (0, step, extent - step)[role]) % extent


def role_code(here, role):
    parity = here % 2
    return (1, 2 * parity, 2 - 2 * parity)[role]


def kernel(cfg, owner_hbm, slot_hbm, table_hbm, star_hbm, inv_hbm, owned_ref, comb_ref,
           owner_ref, slot_ref, table_ref, key_out, src_out, key_ref, src_ref,
           star, inv, made, sent, came, tgt_out, tgt, wide_out, wide,
           pd, px, wp, ry, rx, rw, own, g1, g2, w1, ans,
           index_sem, load_sem, t_send, t_recv, a_send, a_recv, b_send, b_recv, out_send, out_recv, *back):
    nx, ny, nz, chunks, capacity = cfg
    gx, gy, gz = lax.axis_index("gx"), lax.axis_index("gy"), lax.axis_index("gz")
    patch_count, block_count = owner_hbm.shape
    total = patch_count * block_count
    rows, lanes = came.shape[2], came.shape[3]
    steps = offsets(ny)
    ly = len(steps)

    def at(role_x, dy, role_z):
        return (partner(gx, role_x, nx), (gy + dy + ny) % ny, partner(gz, role_z, nz))

    near_x, corner, far_z = at(1, 0, 0), at(2, 0, 0), at(0, 0, 2)
    near_y = ((gx + nx // 2) % nx, gy, gz)

    groups = [[(rz, d, r) for rz in (0, 1) for d in range(ly)] for r in range(3)]
    groups.append([(2, d, r) for r in range(3) for d in range(ly)])
    bases = [2 * ly * r * capacity for r in range(4)]

    def route(part, sign):
        rz, d, r = part
        dy = sign * steps[d]
        return at(r, dy, 0) if rz == 2 else at(0, dy, rz)

    indices = [
        pltpu.make_async_copy(source, target, index_sem.at[i])
        for i, (source, target) in enumerate(
            ((owner_hbm, owner_ref), (slot_hbm, slot_ref), (table_hbm, table_ref)))]
    loads = [pltpu.make_async_copy(star_hbm, star, load_sem.at[patch_count])]
    for p in range(patch_count):
        loads.append(pltpu.make_async_copy(inv_hbm.at[p], inv.at[p], load_sem.at[p]))
    for load in indices + loads[:2]:
        load.start()

    barrier = pltpu.get_barrier_semaphore()
    greeted = [at(0, dy, rz) for dy in steps for rz in (0, 1) if dy or rz]
    greeted += [at(r, dy, 0) for dy in steps for r in (1, 2)] + [far_z, near_y]
    for device in greeted:
        pl.semaphore_signal(barrier, inc=1, device_id=device, device_id_type=MESH)

    for load in indices:
        load.wait()
    for load in loads[2:]:
        load.start()

    owner = owner_ref[...]
    owner_x = sum(((owner >= i * ny * nz).astype(jnp.int32) for i in range(1, nx)), jnp.zeros_like(owner))
    owner = owner - owner_x * (ny * nz)
    owner_y = sum(((owner >= i * nz).astype(jnp.int32) for i in range(1, ny)), jnp.zeros_like(owner))
    role_x = role_of(offset_index(owner_x, gx, nx), gx)
    at_y = offset_index(owner_y, gy, ny)
    role_z = role_of(offset_index(owner - owner_y * nz, gz, nz), gz)
    where = jnp.where(role_z == 2, 6 * ly + role_x * ly + at_y, (2 * role_x + role_z) * ly + at_y)
    key = where * capacity + slot_ref[...]
    key_out[0:patch_count, 0:block_count] = key
    tall = src_out.shape[0]
    number = lax.broadcasted_iota(jnp.int32, (tall, block_count), 0)
    block = lax.broadcasted_iota(jnp.int32, (tall, block_count), 1)
    found = jnp.zeros((tall, block_count), jnp.int32)
    for p in range(patch_count):
        hit = jnp.broadcast_to(key[p:p + 1, :], (tall, block_count)) == number
        found = jnp.maximum(found, jnp.where(hit, block + p * block_count, 0))
    src_out[...] = jnp.broadcast_to(
        jnp.max(found, axis=1, keepdims=True), src_out.shape)
    scalars = [
        pltpu.make_async_copy(key_out, key_ref, index_sem.at[0]),
        pltpu.make_async_copy(src_out, src_ref, index_sem.at[1])]
    for load in scalars:
        load.start()

    def entry(role_x, dy, role_z, s):
        code = 9 * role_code(gx, role_x) + 3 * (dy + 1) + role_code(gz, role_z)
        return jnp.full((1, lanes), table_ref[0, s, code], jnp.int32)

    for g, parts in enumerate(groups):
        for i, (rz, d, r) in enumerate(parts):
            for s in range(capacity):
                j = i * capacity + s
                if g == 3:
                    wide_out[j:j + 1, :] = entry(r, steps[d], rz, s)
                elif g:
                    tgt_out[g, j:j + 1, :] = entry(r, steps[d], rz, s)
                else:
                    tgt[g, j:j + 1, :] = entry(r, steps[d], rz, s)

    loads[0].wait()
    for p in range(patch_count):
        loads[1 + p].wait()
        block = lax.dot_general(
            star[p], inv[p], (((1,), (1,)), ((), ())), preferred_element_type=jnp.float32)
        for b in range(block_count):
            made[p * block_count + b] = block[:, b * lanes:(b + 1) * lanes]

    for load in scalars:
        load.wait()
    pl.semaphore_wait(barrier, len(greeted))

    def launch(source, target, send_sem, recv_sem, device):
        copy = pltpu.make_async_remote_copy(
            src_ref=source, dst_ref=target, send_sem=send_sem, recv_sem=recv_sem,
            device_id=device, device_id_type=MESH)
        copy.start()
        return copy

    t_copies = [
        launch(wide_out, wide, t_send.at[2], t_recv.at[2], far_z),
        launch(tgt_out.at[1], tgt.at[1], t_send.at[0], t_recv.at[0], near_x),
        launch(tgt_out.at[2], tgt.at[2], t_send.at[1], t_recv.at[1], corner),
    ]

    def piece(ref, c, slots):
        return ref[c].at[slots] if isinstance(ref, tuple) else ref.at[c, slots]

    def send_part(source, target, sends, recvs, g, i, c, sign):
        k = bases[g] + i * capacity
        launch(piece(source, c, pl.ds(k, capacity)), piece(target, c, pl.ds(k, capacity)),
               sends.at[g], recvs.at[g, c], route(groups[g][i], sign))

    def await_group(source, target, recvs, g, c):
        many = pl.ds(bases[g] + capacity, (len(groups[g]) - 1) * capacity)
        pltpu.make_async_copy(piece(source, c, many), piece(target, c, many), recvs.at[g, c]).wait()

    def pick(g, i):
        held = sent if i else came
        for s in range(capacity):
            k = bases[g] + i * capacity + s
            n = jnp.clip(src_ref[k, 0], 0, total - 1)
            for c in range(chunks):
                held[c, k] = made[n, c * rows:(c + 1) * rows, :]

    near = [(g, i) for g in (2, 1, 0) for i in range(ly, 2 * ly)]
    wide_parts = [(3, i) for i in reversed(range(1, 3 * ly))]
    beside = [(g, i) for g in (2, 1, 0) for i in range(1, ly)]

    def send_near(c):
        for g, i in near:
            send_part(sent, came, a_send, a_recv, g, i, c, 1)

    for g, i in near:
        pick(g, i)
        send_part(sent, came, a_send, a_recv, g, i, 0, 1)
    for g, i in wide_parts:
        pick(g, i)
        send_part(sent, came, a_send, a_recv, g, i, 0, 1)
    for g, i in beside:
        pick(g, i)
        send_part(sent, came, a_send, a_recv, g, i, 0, 1)
    for g in range(4):
        pick(g, 0)
    ahead = max(1, chunks // 2)
    for c in range(1, chunks):
        if c < ahead:
            send_near(c)
        for g, i in wide_parts + beside:
            send_part(sent, came, a_send, a_recv, g, i, c, 1)

    def where_of(g, j):
        row = wide[j:j + 1, :] if g == 3 else tgt[g, j:j + 1, :]
        return jnp.broadcast_to(row, (8, lanes))

    def reduce(g, c, added, out):
        await_group(sent, came, a_recv, g, c)
        for r in range(rows // 8):
            at_rows = pl.ds(r * 8, 8)
            sums = [None] * OWNB
            for t in range(OWNB):
                for ref in added:
                    value = ref[c, t, at_rows, :]
                    sums[t] = value if sums[t] is None else sums[t] + value
            for j in range(len(groups[g]) * capacity):
                value = came[c, bases[g] + j, at_rows, :]
                where = where_of(g, j)
                for t in range(OWNB):
                    term = jnp.where(where == t, value, 0.0)
                    sums[t] = term if sums[t] is None else sums[t] + term
            for t in range(OWNB):
                out[c, t, at_rows, :] = sums[t]

    def answer(g, c, held):
        for r in range(rows // 8):
            at_rows = pl.ds(r * 8, 8)
            values = [held[c, t, at_rows, :] for t in range(OWNB)]
            for j in range(len(groups[g]) * capacity):
                where = where_of(g, j)
                out = values[0]
                for t in range(1, OWNB):
                    out = jnp.where(where == t, values[t], out)
                into = ans.at[c] if j >= capacity else back[c]
                into[bases[g] + j, at_rows, :] = out
        for i in reversed(range(1, len(groups[g]))):
            send_part(ans, back, b_send, b_recv, g, i, c, -1)

    outs = ((pd, ry, near_y), (px, rx, near_x), (wp, rw, far_z),
            (own, g1, near_x), (g1, g2, near_y), (own, w1, far_z))

    def pass_on(kind, c):
        source, target, device = outs[kind]
        launch(source.at[c], target.at[c], out_send.at[kind], out_recv.at[kind, c], device)

    def await_out(kind, c):
        source, target, _ = outs[kind]
        pltpu.make_async_copy(source.at[c], target.at[c], out_recv.at[kind, c]).wait()

    def sum_proxied(c):
        if c == 0:
            t_copies[0].wait_recv()
        reduce(3, c, [], wp)
        pass_on(2, c)
        if c + ahead < chunks:
            send_near(c + ahead)

    def sum_corner(c):
        if c == 0:
            t_copies[2].wait_recv()
        reduce(2, c, [], pd)
        pass_on(0, c)

    def sum_near(c):
        if c == 0:
            t_copies[1].wait_recv()
        await_out(0, c)
        reduce(1, c, [ry], px)
        pass_on(1, c)

    def sum_own(c):
        await_out(1, c)
        await_out(2, c)
        reduce(0, c, [rx, rw], own)
        pass_on(5, c)
        pass_on(3, c)
        answer(0, c, own)
        for t in range(OWNB):
            owned_ref[t, pl.ds(c * rows, rows), :] = own[c, t]

    def back_near(c):
        await_out(3, c)
        pass_on(4, c)
        answer(1, c, g1)

    def back_proxied(c):
        await_out(5, c)
        answer(3, c, w1)

    def back_corner(c):
        await_out(4, c)
        answer(2, c, g2)

    def finish(c):
        for g in range(4):
            await_group(ans, back, b_recv, g, c)

        def place(p, carry):
            for b in range(block_count):
                comb_ref[p * block_count + b, pl.ds(c * rows, rows), :] = back[c][jnp.clip(key_ref[p, b], 0, came.shape[1] - 1)]
            return carry

        lax.fori_loop(0, patch_count, place, 0)

    plan = [
        (sum_corner, 9.5, 2.8), (sum_proxied, 9.8, 2.1), (sum_near, 13.2, 2.8), (sum_own, 17.0, 3.0),
        (back_near, 20.6, 3.0), (back_proxied, 25.5, 2.1), (back_corner, 24.2, 3.0), (finish, 37.0, 1.0),
    ]
    timed = [(start + every * 4.0 / chunks * c, i, c) for i, (_, start, every) in enumerate(plan) for c in range(chunks)]
    for _, i, c in sorted(timed):
        plan[i][0](c)

    for copy in t_copies:
        copy.wait_send()
    for g, parts in enumerate(groups):
        many = pl.ds(bases[g] + capacity, (len(parts) - 1) * capacity)
        for source, sends in ((sent, a_send), (ans, b_send)):
            pltpu.make_async_copy(source.at[:, many], came.at[:, many], sends.at[g]).wait()
    for kind, (source, target, _) in enumerate(outs):
        pltpu.make_async_copy(source, target, out_send.at[kind]).wait()


def store_kernel(owned_ref, comb_ref, owned_hbm, comb_hbm, sem):
    copies = [
        pltpu.make_async_copy(comb_ref, comb_hbm, sem.at[0]),
        pltpu.make_async_copy(owned_ref, owned_hbm, sem.at[1])]
    for copy in copies:
        copy.start()
    for copy in copies:
        copy.wait()


def on_device(star_residual, patch_inverse, block_owner, block_slot, recv_target):
    nx, ny, nz = lax.axis_size("gx"), lax.axis_size("gy"), lax.axis_size("gz")
    patch_count, rhs_count, patch_order = star_residual.shape
    block_count = block_owner.shape[1]
    width = patch_order // block_count
    capacity = recv_target.shape[2]
    total = patch_count * block_count
    ly = len(offsets(ny))
    slots = 9 * ly * capacity
    tall = -(-slots // 8) * 8
    chunks = CHUNKS
    rows = rhs_count // chunks
    hbm = pl.BlockSpec(memory_space=pltpu.HBM)
    vmem = pl.BlockSpec(memory_space=pltpu.VMEM)
    anywhere = pl.BlockSpec(memory_space=pl.ANY)
    f32, i32 = jnp.float32, jnp.int32
    slotted = pltpu.VMEM((chunks, slots, rows, width), f32)
    targeted = pltpu.VMEM((chunks, OWNB, rows, width), f32)
    table = pltpu.VMEM((3, 2 * ly * capacity, width), i32)
    wide = pltpu.VMEM((3 * ly * capacity, width), i32)
    dma = pltpu.SemaphoreType.DMA
    limit = VMEM_BYTES - SPARE - (OWNB + total) * rhs_count * width * 4
    owned, comb = pl.pallas_call(
        functools.partial(kernel, (nx, ny, nz, chunks, capacity)),
        out_shape=(
            pltpu.VMEM((OWNB, rhs_count, width), f32),
            pltpu.VMEM((total, rhs_count, width), f32),
        ),
        in_specs=[hbm] * 5,
        out_specs=(vmem, vmem),
        scratch_shapes=[
            pltpu.VMEM(block_owner.shape, i32),
            pltpu.VMEM(block_slot.shape, i32),
            pltpu.SMEM((1, capacity, recv_target.shape[1]), i32),
            pltpu.VMEM((8, 128), i32),
            pltpu.VMEM((tall, 128), i32),
            pltpu.SMEM((8, 128), i32),
            pltpu.SMEM((tall, 128), i32),
            pltpu.VMEM(star_residual.shape, star_residual.dtype),
            pltpu.VMEM(patch_inverse.shape, patch_inverse.dtype),
            pltpu.VMEM((total, rhs_count, width), f32),
            slotted, slotted,
            table, table, wide, wide,
            targeted, targeted, targeted, targeted, targeted, targeted, targeted, targeted, targeted, targeted,
            slotted,
            dma((3,)), dma((patch_count + 1,)), dma((3,)), dma((3,)),
            dma((4,)), dma((4, chunks)), dma((4,)), dma((4, chunks)),
            dma((6,)), dma((6, chunks)),
        ] + [pltpu.VMEM((slots, rows, width), f32)] * chunks,
        compiler_params=pltpu.CompilerParams(
            collective_id=0, has_side_effects=True, vmem_limit_bytes=limit),
    )(block_owner, block_slot, recv_target.transpose(0, 2, 1), star_residual, patch_inverse)
    owned, comb = pl.pallas_call(
        store_kernel,
        out_shape=(
            jax.ShapeDtypeStruct((OWNB, rhs_count, width), f32),
            jax.ShapeDtypeStruct((total, rhs_count, width), f32),
        ),
        in_specs=[anywhere, anywhere],
        out_specs=(anywhere, anywhere),
        scratch_shapes=[dma((2,))],
        compiler_params=pltpu.CompilerParams(vmem_limit_bytes=1024 * 1024),
    )(owned, comb)
    return owned, comb.reshape(patch_count, block_count, rhs_count, width)


def solution(mesh):
    placed = (
        P(("gx", "gy", "gz"), None, None),
        P(("gx", "gy", "gz"), None, None),
        P(("gx", "gy", "gz"), None),
        P(("gx", "gy", "gz"), None),
        P(("gx", "gy", "gz"), None, None),
    )
    return jax.shard_map(
        on_device,
        mesh=mesh,
        in_specs=placed,
        out_specs=(P(("gx", "gy", "gz"), None, None), P(("gx", "gy", "gz"), None, None, None)),
        check_vma=False,
    )
```

time: 50.2 us -> 45.3 us (0.902)
  Pallas kernels: 49.3 us -> 44.5 us
    pallas_call x2, Pallas kernels: 49.3 us -> 44.5 us  [the longest x1 43.4 us: on_device(): pl.pallas_call(functools.partial(kernel, (nx, ny, nz, chunks, capacity)),...]
where the time goes in v1:
time: 45.3 us; the launch traced here: 45.1 us
  Pallas kernels  44.5 us (98%)
  between operations  0.64 us (1%)
    pallas_call x1, Pallas kernels, on_device(): pl.pallas_call(functools.partial(kernel, (nx, ny, nz, chunks, capacity)),...  43.4 us
    pallas_call x1, Pallas kernels, on_device(): pl.pallas_call(store_kernel, out_shape=(jax.ShapeDtypeStruct((OWNB, rhs_c...  1.11 us

profile of v1, /device:TPU:0, one launch (start us, length us, event | category | flops | bytes accessed | tf_op | source)
XLA Modules:
  0.0 45.1 jit_solution(14824676811486574820)
XLA Ops:
  0.6 43.4 %shard_map.68 = (f32[8,64,128]{2,1,0:T(8,128)S(1)}, f32[36,64,128]{2,1,0:T(8,128)S(1)}) custom-call(s32[4,9]{1,0:T(4,128)} %owner_hbm.1, s32[4,9]{1,0:T(4,128)} %slot_hbm.1, s32[1,2,27]{2,1,0:T(2,128)} %bitcast.2, bf16[4,64,1152]{2,1,0:T(8,128)(2,1)} %star_hbm.1, bf16[4,1152,1152]{2,1,0:T(8,128)(2,1)} %inv_hbm.1), custom_call_target="tpu_custom_call" | custom-call | tf_op jit(solution)/shard_map/pallas_call | solution.py:353
  44.0 1.1 %shard_map.69 = (f32[8,64,128]{2,1,0:T(8,128)}, f32[36,64,128]{2,1,0:T(8,128)}) custom-call(f32[8,64,128]{2,1,0:T(8,128)S(1)} %get-tuple-element.6.owned_ref, f32[36,64,128]{2,1,0:T(8,128)S(1)} %get-tuple-element.7.comb_ref), custom_call_target="tpu_custom_call" | custom-call | tf_op jit(solution)/shard_map/pallas_call | solution.py:383

commit v2 on v1

--- a/solution.py
+++ b/solution.py
@@ -9,6 +9,8 @@
 
 OWNB = 8
 CHUNKS = 4
+RAW_OUT = 2
+RAW_BACK = 1
 VMEM_BYTES = 67043328
 SPARE = 131072
 MESH = pl.DeviceIdType.MESH
@@ -42,7 +44,8 @@
            owner_ref, slot_ref, table_ref, key_out, src_out, key_ref, src_ref,
            star, inv, made, sent, came, tgt_out, tgt, wide_out, wide,
            pd, px, wp, ry, rx, rw, own, g1, g2, w1, ans,
-           index_sem, load_sem, t_send, t_recv, a_send, a_recv, b_send, b_recv, out_send, out_recv, *back):
+           index_sem, load_sem, t_send, t_recv, a_send, a_recv, b_send, b_recv, out_send, out_recv,
+           f_send, f_recv, e_send, e_recv, *back):
     nx, ny, nz, chunks, capacity = cfg
     gx, gy, gz = lax.axis_index("gx"), lax.axis_index("gy"), lax.axis_index("gz")
     patch_count, block_count = owner_hbm.shape
@@ -60,6 +63,14 @@
     groups = [[(rz, d, r) for rz in (0, 1) for d in range(ly)] for r in range(3)]
     groups.append([(2, d, r) for r in range(3) for d in range(ly)])
     bases = [2 * ly * r * capacity for r in range(4)]
+    raw_out, raw_back = min(RAW_OUT, chunks), chunks - min(RAW_BACK, chunks)
+    inner = (gz > 0) & (gz < nz - 1)
+    outer = jnp.logical_not(inner)
+
+    def far_slots(r):
+        return pl.ds(bases[3] + r * ly * capacity, ly * capacity)
+
+    every_far = pl.ds(bases[3], 3 * ly * capacity)
 
     def route(part, sign):
         rz, d, r = part
@@ -70,22 +81,39 @@
         pltpu.make_async_copy(source, target, index_sem.at[i])
         for i, (source, target) in enumerate(
             ((owner_hbm, owner_ref), (slot_hbm, slot_ref), (table_hbm, table_ref)))]
+    half = block_count // 2 * lanes
     loads = [pltpu.make_async_copy(star_hbm, star, load_sem.at[patch_count])]
-    for p in range(patch_count):
-        loads.append(pltpu.make_async_copy(inv_hbm.at[p], inv.at[p], load_sem.at[p]))
-    for load in indices + loads[:2]:
+    spans = [(0, 0, half), (0, half, block_count * lanes)]
+    spans += [(p, 0, block_count * lanes) for p in range(1, patch_count)]
+    for i, (p, low, high) in enumerate(spans):
+        span = pl.ds(low, high - low)
+        sem = load_sem.at[p if i else patch_count + 1]
+        loads.append(pltpu.make_async_copy(inv_hbm.at[p, span], inv.at[p, span], sem))
+    for load in indices + loads[:3]:
         load.start()
 
     barrier = pltpu.get_barrier_semaphore()
-    greeted = [at(0, dy, rz) for dy in steps for rz in (0, 1) if dy or rz]
-    greeted += [at(r, dy, 0) for dy in steps for r in (1, 2)] + [far_z, near_y]
+    greeted = [at(0, dy, rz) for dy in steps for rz in (0, 1, 2) if dy or rz]
+    greeted += [at(r, dy, 0) for dy in steps for r in (1, 2)] + [near_y]
     for device in greeted:
         pl.semaphore_signal(barrier, inc=1, device_id=device, device_id_type=MESH)
 
     for load in indices:
         load.wait()
-    for load in loads[2:]:
+    for load in loads[3:]:
         load.start()
+
+    def multiply(i):
+        p, low, high = spans[i]
+        loads[1 + i].wait()
+        block = lax.dot_general(
+            star[p], inv[p, low:high, :], (((1,), (1,)), ((), ())), preferred_element_type=jnp.float32)
+        for b in range((high - low) // lanes):
+            made[p * block_count + low // lanes + b] = block[:, b * lanes:(b + 1) * lanes]
+
+    loads[0].wait()
+    multiply(0)
+    multiply(1)
 
     owner = owner_ref[...]
     owner_x = sum(((owner >= i * ny * nz).astype(jnp.int32) for i in range(1, nx)), jnp.zeros_like(owner))
@@ -116,27 +144,21 @@
         code = 9 * role_code(gx, role_x) + 3 * (dy + 1) + role_code(gz, role_z)
         return jnp.full((1, lanes), table_ref[0, s, code], jnp.int32)
 
-    for g, parts in enumerate(groups):
-        for i, (rz, d, r) in enumerate(parts):
-            for s in range(capacity):
-                j = i * capacity + s
-                if g == 3:
-                    wide_out[j:j + 1, :] = entry(r, steps[d], rz, s)
-                elif g:
-                    tgt_out[g, j:j + 1, :] = entry(r, steps[d], rz, s)
-                else:
-                    tgt[g, j:j + 1, :] = entry(r, steps[d], rz, s)
-
-    loads[0].wait()
-    for p in range(patch_count):
-        loads[1 + p].wait()
-        block = lax.dot_general(
-            star[p], inv[p], (((1,), (1,)), ((), ())), preferred_element_type=jnp.float32)
-        for b in range(block_count):
-            made[p * block_count + b] = block[:, b * lanes:(b + 1) * lanes]
-
-    for load in scalars:
-        load.wait()
+    for r in range(3):
+        for rz in range(3):
+            for d, dy in enumerate(steps):
+                for s in range(capacity):
+                    row = entry(r, dy, rz, s)
+                    j = (rz * ly + d) * capacity + s
+                    held = tgt_out if r else tgt
+                    held[r, j:j + 1, :] = row
+                    if rz == 2:
+                        j = (r * ly + d) * capacity + s
+                        wide_out[j:j + 1, :] = row
+
+    for i in range(2, len(spans) - 1):
+        multiply(i)
+
     pl.semaphore_wait(barrier, len(greeted))
 
     def launch(source, target, send_sem, recv_sem, device):
@@ -152,6 +174,10 @@
         launch(tgt_out.at[2], tgt.at[2], t_send.at[1], t_recv.at[1], corner),
     ]
 
+    multiply(len(spans) - 1)
+    for load in scalars:
+        load.wait()
+
     def piece(ref, c, slots):
         return ref[c].at[slots] if isinstance(ref, tuple) else ref.at[c, slots]
 
@@ -165,12 +191,34 @@
         pltpu.make_async_copy(piece(source, c, many), piece(target, c, many), recvs.at[g, c]).wait()
 
     def pick(g, i):
-        held = sent if i else came
         for s in range(capacity):
             k = bases[g] + i * capacity + s
             n = jnp.clip(src_ref[k, 0], 0, total - 1)
             for c in range(chunks):
-                held[c, k] = made[n, c * rows:(c + 1) * rows, :]
+                value = made[n, c * rows:(c + 1) * rows, :]
+                if i or (g == 3 and c < raw_out):
+                    sent[c, k] = value
+                if not i:
+                    if g == 3 and c < raw_out:
+                        @pl.when(outer)
+                        def _():
+                            came[c, k] = value
+                    else:
+                        came[c, k] = value
+
+    def send_far(c):
+        @pl.when(inner)
+        def _():
+            for r in (2, 1, 0):
+                for d in reversed(range(ly)):
+                    k = pl.ds(bases[3] + (r * ly + d) * capacity, capacity)
+                    launch(sent.at[c, k], came.at[c, k], f_send, f_recv.at[r, c], at(0, steps[d], 2))
+
+        @pl.when(outer)
+        def _():
+            for g, i in wide_parts:
+                k = pl.ds(bases[g] + i * capacity, capacity)
+                launch(sent.at[c, k], came.at[c, k], f_send, a_recv.at[g, c], route(groups[g][i], 1))
 
     near = [(g, i) for g in (2, 1, 0) for i in range(ly, 2 * ly)]
     wide_parts = [(3, i) for i in reversed(range(1, 3 * ly))]
@@ -183,19 +231,25 @@
     for g, i in near:
         pick(g, i)
         send_part(sent, came, a_send, a_recv, g, i, 0, 1)
-    for g, i in wide_parts:
+    for g, i in wide_parts + [(3, 0)]:
         pick(g, i)
-        send_part(sent, came, a_send, a_recv, g, i, 0, 1)
+    if raw_out:
+        send_far(0)
+    else:
+        for g, i in wide_parts:
+            send_part(sent, came, a_send, a_recv, g, i, 0, 1)
     for g, i in beside:
         pick(g, i)
         send_part(sent, came, a_send, a_recv, g, i, 0, 1)
-    for g in range(4):
+    for g in range(3):
         pick(g, 0)
     ahead = max(1, chunks // 2)
     for c in range(1, chunks):
         if c < ahead:
             send_near(c)
-        for g, i in wide_parts + beside:
+        if c < raw_out:
+            send_far(c)
+        for g, i in ([] if c < raw_out else wide_parts) + beside:
             send_part(sent, came, a_send, a_recv, g, i, c, 1)
 
     def where_of(g, j):
@@ -220,7 +274,55 @@
             for t in range(OWNB):
                 out[c, t, at_rows, :] = sums[t]
 
+    def add_far(g, c, out):
+        pltpu.make_async_copy(sent.at[c, far_slots(g)], came.at[c, far_slots(g)], f_recv.at[g, c]).wait()
+        for r in range(rows // 8):
+            at_rows = pl.ds(r * 8, 8)
+            sums = [out[c, t, at_rows, :] for t in range(OWNB)]
+            for j in range(ly * capacity):
+                value = came[c, bases[3] + g * ly * capacity + j, at_rows, :]
+                where = where_of(g, 2 * ly * capacity + j)
+                for t in range(OWNB):
+                    sums[t] = sums[t] + jnp.where(where == t, value, 0.0)
+            for t in range(OWNB):
+                out[c, t, at_rows, :] = sums[t]
+
+    def sum_role(g, c, added, out):
+        reduce(g, c, added, out)
+        if c < raw_out:
+            @pl.when(inner)
+            def _():
+                add_far(g, c, out)
+
+    def answer_far(g, c, held):
+        for r in range(rows // 8):
+            at_rows = pl.ds(r * 8, 8)
+            values = [held[c, t, at_rows, :] for t in range(OWNB)]
+            for j in range(ly * capacity):
+                where = where_of(g, 2 * ly * capacity + j)
+                out = values[0]
+                for t in range(1, OWNB):
+                    out = jnp.where(where == t, values[t], out)
+                ans[c, bases[3] + g * ly * capacity + j, at_rows, :] = out
+        for d in reversed(range(ly)):
+            k = pl.ds(bases[3] + (g * ly + d) * capacity, capacity)
+            launch(ans.at[c, k], back[c].at[k], e_send, e_recv.at[c], at(0, -steps[d], 2))
+
     def answer(g, c, held):
+        if g < 3 and c >= raw_back:
+            answer_part(g, c, held)
+
+            @pl.when(inner)
+            def _():
+                answer_far(g, c, held)
+        elif g == 3 and c >= raw_back:
+            @pl.when(outer)
+            def _():
+                answer_part(g, c, held)
+        else:
+            answer_part(g, c, held)
+
+    def answer_part(g, c, held):
         for r in range(rows // 8):
             at_rows = pl.ds(r * 8, 8)
             values = [held[c, t, at_rows, :] for t in range(OWNB)]
@@ -248,29 +350,47 @@
     def sum_proxied(c):
         if c == 0:
             t_copies[0].wait_recv()
-        reduce(3, c, [], wp)
-        pass_on(2, c)
+
+        def proxy():
+            reduce(3, c, [], wp)
+            pass_on(2, c)
+
+        if c < raw_out:
+            pl.when(outer)(proxy)
+        else:
+            proxy()
         if c + ahead < chunks:
             send_near(c + ahead)
 
     def sum_corner(c):
         if c == 0:
             t_copies[2].wait_recv()
-        reduce(2, c, [], pd)
+        sum_role(2, c, [], pd)
         pass_on(0, c)
 
     def sum_near(c):
         if c == 0:
             t_copies[1].wait_recv()
         await_out(0, c)
-        reduce(1, c, [ry], px)
+        sum_role(1, c, [ry], px)
         pass_on(1, c)
 
     def sum_own(c):
         await_out(1, c)
-        await_out(2, c)
-        reduce(0, c, [rx, rw], own)
-        pass_on(5, c)
+        if c < raw_out:
+            sum_role(0, c, [rx], own)
+
+            @pl.when(outer)
+            def _():
+                await_out(2, c)
+                own[c] = own[c] + rw[c]
+        else:
+            await_out(2, c)
+            reduce(0, c, [rx, rw], own)
+        if c >= raw_back:
+            pl.when(outer)(lambda: pass_on(5, c))
+        else:
+            pass_on(5, c)
         pass_on(3, c)
         answer(0, c, own)
         for t in range(OWNB):
@@ -282,16 +402,30 @@
         answer(1, c, g1)
 
     def back_proxied(c):
-        await_out(5, c)
-        answer(3, c, w1)
+        if c >= raw_back:
+            @pl.when(outer)
+            def _():
+                await_out(5, c)
+                answer_part(3, c, w1)
+        else:
+            await_out(5, c)
+            answer_part(3, c, w1)
 
     def back_corner(c):
         await_out(4, c)
         answer(2, c, g2)
 
     def finish(c):
-        for g in range(4):
+        for g in range(3):
             await_group(ans, back, b_recv, g, c)
+        if c >= raw_back:
+            pl.when(outer)(lambda: await_group(ans, back, b_recv, 3, c))
+
+            @pl.when(inner)
+            def _():
+                pltpu.make_async_copy(ans.at[c, every_far], back[c].at[every_far], e_recv.at[c]).wait()
+        else:
+            await_group(ans, back, b_recv, 3, c)
 
         def place(p, carry):
             for b in range(block_count):
@@ -300,22 +434,55 @@
 
         lax.fori_loop(0, patch_count, place, 0)
 
+    def drain(ref, low, high, slots, sem):
+        if high > low:
+            view = ref.at[pl.ds(low, high - low)] if slots is None else ref.at[pl.ds(low, high - low), slots]
+            pltpu.make_async_copy(view, view, sem).wait()
+
+    def drain_sums():
+        for copy in t_copies:
+            copy.wait_send()
+        for g, parts in enumerate(groups):
+            many = pl.ds(bases[g] + capacity, (len(parts) - 1) * capacity)
+            drain(sent, raw_out if g == 3 else 0, chunks, many, a_send.at[g])
+        pl.when(inner)(lambda: drain(sent, 0, raw_out, every_far, f_send))
+        pl.when(outer)(lambda: drain(sent, 0, raw_out, many, f_send))
+        for kind, (source, _, _) in enumerate(outs):
+            if kind in (2, 5):
+                low, high = (raw_out, chunks) if kind == 2 else (0, raw_back)
+                pl.when(inner)(lambda: drain(source, low, high, None, out_send.at[kind]))
+                pl.when(outer)(lambda: drain(source, 0, chunks, None, out_send.at[kind]))
+            else:
+                drain(source, 0, chunks, None, out_send.at[kind])
+
     plan = [
         (sum_corner, 9.5, 2.8), (sum_proxied, 9.8, 2.1), (sum_near, 13.2, 2.8), (sum_own, 17.0, 3.0),
-        (back_near, 20.6, 3.0), (back_proxied, 25.5, 2.1), (back_corner, 24.2, 3.0), (finish, 37.0, 1.0),
+        (back_near, 20.6, 3.0), (back_proxied, 30.5, 2.1), (back_corner, 24.2, 3.0), (finish, 37.0, 1.0),
     ]
     timed = [(start + every * 4.0 / chunks * c, i, c) for i, (_, start, every) in enumerate(plan) for c in range(chunks)]
     for _, i, c in sorted(timed):
+        if (i, c) == (len(plan) - 1, chunks - 1):
+            drain_sums()
         plan[i][0](c)
 
-    for copy in t_copies:
-        copy.wait_send()
+    def drain(ref, low, high, slots, sem):
+        if high > low:
+            view = ref.at[pl.ds(low, high - low)] if slots is None else ref.at[pl.ds(low, high - low), slots]
+            pltpu.make_async_copy(view, view, sem).wait()
+
     for g, parts in enumerate(groups):
         many = pl.ds(bases[g] + capacity, (len(parts) - 1) * capacity)
-        for source, sends in ((sent, a_send), (ans, b_send)):
-            pltpu.make_async_copy(source.at[:, many], came.at[:, many], sends.at[g]).wait()
-    for kind, (source, target, _) in enumerate(outs):
-        pltpu.make_async_copy(source, target, out_send.at[kind]).wait()
+        if g < 3:
+            drain(ans, 0, chunks, many, b_send.at[g])
+        else:
+            @pl.when(inner)
+            def _():
+                drain(ans, 0, raw_back, many, b_send.at[3])
+                drain(ans, raw_back, chunks, every_far, e_send)
+
+            @pl.when(outer)
+            def _():
+                drain(ans, 0, chunks, many, b_send.at[3])
 
 
 def store_kernel(owned_ref, comb_ref, owned_hbm, comb_hbm, sem):
@@ -346,7 +513,7 @@
     f32, i32 = jnp.float32, jnp.int32
     slotted = pltpu.VMEM((chunks, slots, rows, width), f32)
     targeted = pltpu.VMEM((chunks, OWNB, rows, width), f32)
-    table = pltpu.VMEM((3, 2 * ly * capacity, width), i32)
+    table = pltpu.VMEM((3, 3 * ly * capacity, width), i32)
     wide = pltpu.VMEM((3 * ly * capacity, width), i32)
     dma = pltpu.SemaphoreType.DMA
     limit = VMEM_BYTES - SPARE - (OWNB + total) * rhs_count * width * 4
@@ -373,9 +540,10 @@
             table, table, wide, wide,
             targeted, targeted, targeted, targeted, targeted, targeted, targeted, targeted, targeted, targeted,
             slotted,
-            dma((3,)), dma((patch_count + 1,)), dma((3,)), dma((3,)),
+            dma((3,)), dma((patch_count + 2,)), dma((3,)), dma((3,)),
             dma((4,)), dma((4, chunks)), dma((4,)), dma((4, chunks)),
             dma((6,)), dma((6, chunks)),
+            dma, dma((3, chunks)), dma, dma((chunks,)),
         ] + [pltpu.VMEM((slots, rows, width), f32)] * chunks,
         compiler_params=pltpu.CompilerParams(
             collective_id=0, has_side_effects=True, vmem_limit_bytes=limit),

time: 45.3 us -> 43.6 us (0.962)
  Pallas kernels: 44.5 us -> 42.7 us
    pallas_call x1, Pallas kernels: 43.4 us -> 41.6 us  [on_device(): pl.pallas_call(functools.partial(kernel, (nx, ny, nz, chunks, capacity)),...]
where the time goes in v2:
time: 43.6 us; the launch traced here: 43.4 us
  Pallas kernels  42.7 us (98%)
  between operations  0.64 us (1%)
    pallas_call x1, Pallas kernels, on_device(): pl.pallas_call(functools.partial(kernel, (nx, ny, nz, chunks, capacity)),...  41.6 us
    pallas_call x1, Pallas kernels, on_device(): pl.pallas_call(store_kernel, out_shape=(jax.ShapeDtypeStruct((OWNB, rhs_c...  1.11 us

profile of v2, /device:TPU:0, one launch (start us, length us, event | category | flops | bytes accessed | tf_op | source)
XLA Modules:
  0.0 43.4 jit_solution(12471101117728909211)
XLA Ops:
  0.6 41.6 %shard_map.68 = (f32[8,64,128]{2,1,0:T(8,128)S(1)}, f32[36,64,128]{2,1,0:T(8,128)S(1)}) custom-call(s32[4,9]{1,0:T(4,128)} %owner_hbm.1, s32[4,9]{1,0:T(4,128)} %slot_hbm.1, s32[1,2,27]{2,1,0:T(2,128)} %bitcast.2, bf16[4,64,1152]{2,1,0:T(8,128)(2,1)} %star_hbm.1, bf16[4,1152,1152]{2,1,0:T(8,128)(2,1)} %inv_hbm.1), custom_call_target="tpu_custom_call" | custom-call | tf_op jit(solution)/shard_map/pallas_call | solution.py:520
  42.3 1.1 %shard_map.69 = (f32[8,64,128]{2,1,0:T(8,128)}, f32[36,64,128]{2,1,0:T(8,128)}) custom-call(f32[8,64,128]{2,1,0:T(8,128)S(1)} %get-tuple-element.6.owned_ref, f32[36,64,128]{2,1,0:T(8,128)S(1)} %get-tuple-element.7.comb_ref), custom_call_target="tpu_custom_call" | custom-call | tf_op jit(solution)/shard_map/pallas_call | solution.py:551

commit v3 on v2

--- a/solution.py
+++ b/solution.py
@@ -9,8 +9,13 @@
 
 OWNB = 8
 CHUNKS = 4
+EARLY_N = 3.5
+EARLY_O = 2.5
+EARLY_C = 3.0
 RAW_OUT = 2
-RAW_BACK = 1
+RAW_BACK = 2
+STRAIGHT_OUT = 1
+STRAIGHT_BACK = 1
 VMEM_BYTES = 67043328
 SPARE = 131072
 MESH = pl.DeviceIdType.MESH
@@ -339,8 +344,14 @@
     outs = ((pd, ry, near_y), (px, rx, near_x), (wp, rw, far_z),
             (own, g1, near_x), (g1, g2, near_y), (own, w1, far_z))
 
+    straight_out, straight_back = chunks - min(STRAIGHT_OUT, chunks), chunks - min(STRAIGHT_BACK, chunks)
+
     def pass_on(kind, c):
         source, target, device = outs[kind]
+        if kind == 0 and c >= straight_out:
+            device = corner
+        if kind == 4 and c >= straight_back:
+            source, device = own, corner
         launch(source.at[c], target.at[c], out_send.at[kind], out_recv.at[kind, c], device)
 
     def await_out(kind, c):
@@ -371,14 +382,19 @@
     def sum_near(c):
         if c == 0:
             t_copies[1].wait_recv()
-        await_out(0, c)
-        sum_role(1, c, [ry], px)
+        if c < straight_out:
+            await_out(0, c)
+        sum_role(1, c, [ry] if c < straight_out else [], px)
         pass_on(1, c)
 
     def sum_own(c):
         await_out(1, c)
+        added = [rx]
+        if c >= straight_out:
+            await_out(0, c)
+            added = [rx, ry]
         if c < raw_out:
-            sum_role(0, c, [rx], own)
+            sum_role(0, c, added, own)
 
             @pl.when(outer)
             def _():
@@ -386,19 +402,22 @@
                 own[c] = own[c] + rw[c]
         else:
             await_out(2, c)
-            reduce(0, c, [rx, rw], own)
+            reduce(0, c, added + [rw], own)
         if c >= raw_back:
             pl.when(outer)(lambda: pass_on(5, c))
         else:
             pass_on(5, c)
         pass_on(3, c)
+        if c >= straight_back:
+            pass_on(4, c)
         answer(0, c, own)
         for t in range(OWNB):
             owned_ref[t, pl.ds(c * rows, rows), :] = own[c, t]
 
     def back_near(c):
         await_out(3, c)
-        pass_on(4, c)
+        if c < straight_back:
+            pass_on(4, c)
         answer(1, c, g1)
 
     def back_proxied(c):
@@ -457,9 +476,17 @@
 
     plan = [
         (sum_corner, 9.5, 2.8), (sum_proxied, 9.8, 2.1), (sum_near, 13.2, 2.8), (sum_own, 17.0, 3.0),
-        (back_near, 20.6, 3.0), (back_proxied, 30.5, 2.1), (back_corner, 24.2, 3.0), (finish, 37.0, 1.0),
+        (back_near, 20.6, 3.0), (back_proxied, 26.0, 2.1), (back_corner, 24.2, 3.0), (finish, 37.0, 1.0),
     ]
     timed = [(start + every * 4.0 / chunks * c, i, c) for i, (_, start, every) in enumerate(plan) for c in range(chunks)]
+    early = {}
+    for c in range(chunks):
+        out, back_ = c >= straight_out, c >= straight_back
+        early[2, c] = EARLY_N if out else 0.0
+        early[3, c] = EARLY_O if out else 0.0
+        early[4, c] = early[3, c]
+        early[6, c] = early[3, c] + (EARLY_C if back_ else 0.0)
+    timed = [(when - early.get((i, c), 0.0), i, c) for when, i, c in timed]
     for _, i, c in sorted(timed):
         if (i, c) == (len(plan) - 1, chunks - 1):
             drain_sums()

time: 43.6 us -> 42.2 us (0.968)
  Pallas kernels: 42.7 us -> 41.4 us
    pallas_call x1, Pallas kernels: 41.6 us -> 40.3 us  [on_device(): pl.pallas_call(functools.partial(kernel, (nx, ny, nz, chunks, capacity)),...]
where the time goes in v3:
time: 42.2 us; the launch traced here: 42 us
  Pallas kernels  41.4 us (98%)
  between operations  0.64 us (2%)
    pallas_call x1, Pallas kernels, on_device(): pl.pallas_call(functools.partial(kernel, (nx, ny, nz, chunks, capacity)),...  40.3 us
    pallas_call x1, Pallas kernels, on_device(): pl.pallas_call(store_kernel, out_shape=(jax.ShapeDtypeStruct((OWNB, rhs_c...  1.11 us

profile of v3, /device:TPU:0, one launch (start us, length us, event | category | flops | bytes accessed | tf_op | source)
XLA Modules:
  0.0 42.0 jit_solution(10375704205937495803)
XLA Ops:
  0.6 40.3 %shard_map.68 = (f32[8,64,128]{2,1,0:T(8,128)S(1)}, f32[36,64,128]{2,1,0:T(8,128)S(1)}) custom-call(s32[4,9]{1,0:T(4,128)} %owner_hbm.1, s32[4,9]{1,0:T(4,128)} %slot_hbm.1, s32[1,2,27]{2,1,0:T(2,128)} %bitcast.2, bf16[4,64,1152]{2,1,0:T(8,128)(2,1)} %star_hbm.1, bf16[4,1152,1152]{2,1,0:T(8,128)(2,1)} %inv_hbm.1), custom_call_target="tpu_custom_call" | custom-call | tf_op jit(solution)/shard_map/pallas_call | solution.py:547
  40.9 1.1 %shard_map.69 = (f32[8,64,128]{2,1,0:T(8,128)}, f32[36,64,128]{2,1,0:T(8,128)}) custom-call(f32[8,64,128]{2,1,0:T(8,128)S(1)} %get-tuple-element.6.owned_ref, f32[36,64,128]{2,1,0:T(8,128)S(1)} %get-tuple-element.7.comb_ref), custom_call_target="tpu_custom_call" | custom-call | tf_op jit(solution)/shard_map/pallas_call | solution.py:578

commit v4 on v3

--- a/solution.py
+++ b/solution.py
@@ -476,7 +476,7 @@
 
     plan = [
         (sum_corner, 9.5, 2.8), (sum_proxied, 9.8, 2.1), (sum_near, 13.2, 2.8), (sum_own, 17.0, 3.0),
-        (back_near, 20.6, 3.0), (back_proxied, 26.0, 2.1), (back_corner, 24.2, 3.0), (finish, 37.0, 1.0),
+        (back_near, 20.6, 3.0), (back_proxied, 25.5, 1.9), (back_corner, 24.2, 3.0), (finish, 37.0, 1.0),
     ]
     timed = [(start + every * 4.0 / chunks * c, i, c) for i, (_, start, every) in enumerate(plan) for c in range(chunks)]
     early = {}

time: 42.2 us -> 42.2 us (level)
  no operation moved by 1% of the time
where the time goes in v4:
time: 42.2 us; the launch traced here: 42 us
  Pallas kernels  41.3 us (98%)
  between operations  0.64 us (2%)
    pallas_call x1, Pallas kernels, on_device(): pl.pallas_call(functools.partial(kernel, (nx, ny, nz, chunks, capacity)),...  40.2 us
    pallas_call x1, Pallas kernels, on_device(): pl.pallas_call(store_kernel, out_shape=(jax.ShapeDtypeStruct((OWNB, rhs_c...  1.11 us

profile of v4, /device:TPU:0, one launch (start us, length us, event | category | flops | bytes accessed | tf_op | source)
XLA Modules:
  0.0 42.0 jit_solution(1663529329420984494)
XLA Ops:
  0.6 40.2 %shard_map.68 = (f32[8,64,128]{2,1,0:T(8,128)S(1)}, f32[36,64,128]{2,1,0:T(8,128)S(1)}) custom-call(s32[4,9]{1,0:T(4,128)} %owner_hbm.1, s32[4,9]{1,0:T(4,128)} %slot_hbm.1, s32[1,2,27]{2,1,0:T(2,128)} %bitcast.2, bf16[4,64,1152]{2,1,0:T(8,128)(2,1)} %star_hbm.1, bf16[4,1152,1152]{2,1,0:T(8,128)(2,1)} %inv_hbm.1), custom_call_target="tpu_custom_call" | custom-call | tf_op jit(solution)/shard_map/pallas_call | solution.py:547
  40.9 1.1 %shard_map.69 = (f32[8,64,128]{2,1,0:T(8,128)}, f32[36,64,128]{2,1,0:T(8,128)}) custom-call(f32[8,64,128]{2,1,0:T(8,128)S(1)} %get-tuple-element.6.owned_ref, f32[36,64,128]{2,1,0:T(8,128)S(1)} %get-tuple-element.7.comb_ref), custom_call_target="tpu_custom_call" | custom-call | tf_op jit(solution)/shard_map/pallas_call | solution.py:578
